TPU v7x, 128 devices: a whole 4x4x4 slice. The times are simulated.
128 devices in a mesh: rep: 2 (over core), fsdp: 64 (over z, y, x).
Axes of the slice: x: 4, y: 4, z: 4, core: 2. Of those that a mesh axis runs over, the one named last changes fastest.
Arguments:
- x_tokens: bfloat16 [768, 197, 1024], P(('rep', 'fsdp'))
- grad_z: bfloat16 [768, 197, 1024], P(('rep', 'fsdp'))
- w_qkv: float32 [1024, 3072], P('fsdp')
- b_qkv: float32 [3072], P('fsdp')
- w_out: float32 [1024, 1024], P('fsdp')
- w_up: float32 [1024, 4096], P('fsdp')
- b_up: float32 [4096], P('fsdp')
- w_down: float32 [4096, 1024], P('fsdp')
- vec_params: float32 [8, 1024], P(None, 'fsdp')
Outputs:
- output 1: bfloat16 [768, 197, 1024], P(('rep', 'fsdp'))
- output 2: bfloat16 [768, 197, 1024], P(('rep', 'fsdp'))
- output 3: float32 [1024, 3072], P('fsdp')
- output 4: float32 [3072], P('fsdp')
- output 5: float32 [1024, 1024], P('fsdp')
- output 6: float32 [1024, 4096], P('fsdp')
- output 7: float32 [4096], P('fsdp')
- output 8: float32 [4096, 1024], P('fsdp')
- output 9: float32 [8, 1024], P(None, 'fsdp')
All inputs are finite; a program needn't handle non-finite values.
Results may differ from a plain program's by a relative error of at most 0.02.
Values are sent between devices in bfloat16 or wider.
A program may use at most 1 GiB of HBM per device.

v0:
```python
import jax
import jax.numpy as jnp
from jax import lax
from jax.sharding import PartitionSpec as P

HEADS = 16
LN_EPS = 1e-5


def normalize(t):
    mean = jnp.mean(t, axis=-1, keepdims=True)
    centered = t - mean
    variance = jnp.mean(centered * centered, axis=-1, keepdims=True)
    return centered * lax.rsqrt(variance + LN_EPS)


def gelu_exact(t):
    return jax.nn.gelu(t, approximate=False)


def layer_forward(x_loc, weights):
    w_qkv, b_qkv, w_out, w_up, b_up, w_down, vec_rows = weights
    ln1_gain, ln1_bias, out_bias, scale_attn, ln2_gain, ln2_bias, down_bias, scale_mlp = vec_rows
    num_seqs, tokens, width = x_loc.shape
    head_dim = width // HEADS
    score_scale = head_dim ** -0.5
    x_float = x_loc.astype(jnp.float32)
    h_one = (normalize(x_float) * ln1_gain + ln1_bias).astype(jnp.bfloat16)
    qkv_proj = jnp.einsum("std,de->ste", h_one, w_qkv, preferred_element_type=jnp.float32) + b_qkv
    qkv_heads = qkv_proj.astype(jnp.bfloat16).reshape(num_seqs, tokens, 3, HEADS, head_dim)
    q_heads = qkv_heads[:, :, 0]
    k_heads = qkv_heads[:, :, 1]
    v_heads = qkv_heads[:, :, 2]
    scores = jnp.einsum("sqhe,skhe->shqk", q_heads, k_heads, preferred_element_type=jnp.float32) * score_scale
    attn_probs = jax.nn.softmax(scores, axis=-1)
    probs_bf = attn_probs.astype(jnp.bfloat16)
    head_out = jnp.einsum("shqk,skhe->sqhe", probs_bf, v_heads, preferred_element_type=jnp.float32)
    head_out = head_out.astype(jnp.bfloat16).reshape(num_seqs, tokens, width)
    att_out = jnp.einsum("std,de->ste", head_out, w_out, preferred_element_type=jnp.float32) + out_bias
    resid_mid = x_float + scale_attn * att_out
    h_two = (normalize(resid_mid) * ln2_gain + ln2_bias).astype(jnp.bfloat16)
    pre_act = jnp.einsum("std,df->stf", h_two, w_up, preferred_element_type=jnp.float32) + b_up
    mlp_act = gelu_exact(pre_act).astype(jnp.bfloat16)
    mlp_out = jnp.einsum("stf,fd->std", mlp_act, w_down, preferred_element_type=jnp.float32) + down_bias
    z_loc = (resid_mid + scale_mlp * mlp_out).astype(jnp.bfloat16)
    saved = (h_one, qkv_heads, attn_probs, probs_bf, head_out, att_out, resid_mid, h_two, pre_act, mlp_act, mlp_out)
    return z_loc, saved


def layer_backward(x_loc, dz_loc, saved, weights):
    w_qkv, b_qkv, w_out, w_up, b_up, w_down, vec_rows = weights
    ln1_gain, ln1_bias, out_bias, scale_attn, ln2_gain, ln2_bias, down_bias, scale_mlp = vec_rows
    h_one, qkv_heads, attn_probs, probs_bf, head_out, att_out, resid_mid, h_two, pre_act, mlp_act, mlp_out = saved
    num_seqs, tokens, width = x_loc.shape
    head_dim = width // HEADS
    score_scale = head_dim ** -0.5
    g_out = dz_loc.astype(jnp.float32)
    grad_scale_mlp = jnp.sum(g_out * mlp_out, axis=(0, 1))
    d_mlp = g_out * scale_mlp
    grad_down_bias = jnp.sum(d_mlp, axis=(0, 1))
    d_mlp_bf = d_mlp.astype(jnp.bfloat16)
    grad_w_down = jnp.einsum("stf,std->fd", mlp_act, d_mlp_bf, preferred_element_type=jnp.float32)
    d_act = jnp.einsum("std,fd->stf", d_mlp_bf, w_down, preferred_element_type=jnp.float32)
    d_pre = jax.vjp(gelu_exact, pre_act)[1](d_act)[0]
    grad_b_up = jnp.sum(d_pre, axis=(0, 1))
    d_pre_bf = d_pre.astype(jnp.bfloat16)
    grad_w_up = jnp.einsum("std,stf->df", h_two, d_pre_bf, preferred_element_type=jnp.float32)
    d_h_two = jnp.einsum("stf,df->std", d_pre_bf, w_up, preferred_element_type=jnp.float32)
    array_b8, norm_two_back = jax.vjp(normalize, resid_mid)
    grad_ln2_gain = jnp.sum(d_h_two * array_b8, axis=(0, 1))
    grad_ln2_bias = jnp.sum(d_h_two, axis=(0, 1))
    g_resid = g_out + norm_two_back(d_h_two * ln2_gain)[0]
    grad_scale_attn = jnp.sum(g_resid * att_out, axis=(0, 1))
    d_att = g_resid * scale_attn
    grad_out_bias = jnp.sum(d_att, axis=(0, 1))
    d_att_bf = d_att.astype(jnp.bfloat16)
    grad_w_out = jnp.einsum("std,ste->de", head_out, d_att_bf, preferred_element_type=jnp.float32)
    d_heads = jnp.einsum("ste,de->std", d_att_bf, w_out, preferred_element_type=jnp.float32)
    d_heads = d_heads.astype(jnp.bfloat16).reshape(num_seqs, tokens, HEADS, head_dim)
    q_heads = qkv_heads[:, :, 0]
    k_heads = qkv_heads[:, :, 1]
    v_heads = qkv_heads[:, :, 2]
    d_probs = jnp.einsum("sqhe,skhe->shqk", d_heads, v_heads, preferred_element_type=jnp.float32)
    grad_v = jnp.einsum("shqk,sqhe->skhe", probs_bf, d_heads, preferred_element_type=jnp.float32)
    d_scores = attn_probs * (d_probs - jnp.sum(d_probs * attn_probs, axis=-1, keepdims=True))
    d_scores_bf = (d_scores * score_scale).astype(jnp.bfloat16)
    grad_q = jnp.einsum("shqk,skhe->sqhe", d_scores_bf, k_heads, preferred_element_type=jnp.float32)
    grad_k = jnp.einsum("shqk,sqhe->skhe", d_scores_bf, q_heads, preferred_element_type=jnp.float32)
    d_qkv = jnp.stack([grad_q, grad_k, grad_v], axis=2).reshape(num_seqs, tokens, 3 * width)
    grad_b_qkv = jnp.sum(d_qkv, axis=(0, 1))
    d_qkv_bf = d_qkv.astype(jnp.bfloat16)
    grad_w_qkv = jnp.einsum("std,ste->de", h_one, d_qkv_bf, preferred_element_type=jnp.float32)
    d_h_one = jnp.einsum("ste,de->std", d_qkv_bf, w_qkv, preferred_element_type=jnp.float32)
    value_a8, norm_one_back = jax.vjp(normalize, x_loc.astype(jnp.float32))
    grad_ln1_gain = jnp.sum(d_h_one * value_a8, axis=(0, 1))
    grad_ln1_bias = jnp.sum(d_h_one, axis=(0, 1))
    dx_loc = (g_resid + norm_one_back(d_h_one * ln1_gain)[0]).astype(jnp.bfloat16)
    grad_vec = jnp.stack([grad_ln1_gain, grad_ln1_bias, grad_out_bias, grad_scale_attn,
                          grad_ln2_gain, grad_ln2_bias, grad_down_bias, grad_scale_mlp])
    return dx_loc, (grad_w_qkv, grad_b_qkv, grad_w_out, grad_w_up, grad_b_up, grad_w_down, grad_vec)


def gather_weights(shards):
    w_qkv, b_qkv, w_out, w_up, b_up, w_down, vec_params = shards

    def full_rows(shard):
        return lax.all_gather(shard.astype(jnp.bfloat16), "fsdp", axis=0, tiled=True)

    vec_full = lax.all_gather(vec_params.astype(jnp.bfloat16), "fsdp", axis=1, tiled=True)
    return (full_rows(w_qkv), full_rows(b_qkv).astype(jnp.float32), full_rows(w_out), full_rows(w_up),
            full_rows(b_up).astype(jnp.float32), full_rows(w_down), vec_full.astype(jnp.float32))


def reduce_grads(local_grads):
    grad_w_qkv, grad_b_qkv, grad_w_out, grad_w_up, grad_b_up, grad_w_down, grad_vec = local_grads

    def total_rows(full):
        return lax.psum(lax.psum_scatter(full, "fsdp", scatter_dimension=0, tiled=True), "rep")

    vec_total = lax.psum(lax.psum_scatter(grad_vec, "fsdp", scatter_dimension=1, tiled=True), "rep")
    return (total_rows(grad_w_qkv), total_rows(grad_b_qkv), total_rows(grad_w_out), total_rows(grad_w_up),
            total_rows(grad_b_up), total_rows(grad_w_down), vec_total)


def solution(mesh):
    batch_spec = P(("rep", "fsdp"), None, None)
    row_spec = P("fsdp", None)
    flat_spec = P("fsdp")
    col_spec = P(None, "fsdp")
    param_specs = (row_spec, flat_spec, row_spec, row_spec, flat_spec, row_spec, col_spec)

    def device_step(x_loc, dz_loc, w_qkv, b_qkv, w_out, w_up, b_up, w_down, vec_params):
        shards = (w_qkv, b_qkv, w_out, w_up, b_up, w_down, vec_params)
        weights_fwd = gather_weights(shards)
        z_loc, saved = layer_forward(x_loc, weights_fwd)
        shards_bwd = lax.optimization_barrier((shards, z_loc))[0]
        weights_bwd = gather_weights(shards_bwd)
        dx_loc, local_grads = layer_backward(x_loc, dz_loc, saved, weights_bwd)
        return (z_loc, dx_loc) + reduce_grads(local_grads)

    return jax.shard_map(device_step, mesh=mesh, in_specs=(batch_spec, batch_spec) + param_specs,
                         out_specs=(batch_spec, batch_spec) + param_specs, check_vma=False)
```

profile of v0, /device:TPU:1, one launch (start us, length us, event | category | flops | bytes accessed | tf_op | source)
XLA Modules:
  0.0 2749.5 jit_solution(12033703263963248144)
XLA Ops:
  19.3 151.8 %all-gather = bf16[64,16,8]{1,2,0:T(8,128)(2,1)S(1)} all-gather(bf16[1,16,8]{1,2,0:T(8,128)(2,1)S(1)} %convert_bitcast_fusion.1), channel_id=1, replica_groups=mesh['rep'=2,'fsdp'=64] {'fsdp'}, dimensions={0}, use_global_device_ids=true | all-gather | bytes 16640 | tf_op jit(solution)/shard_map/all_gather | solution.py:109
  174.0 287.5 %all-reduce.7 = (bf16[3072]{0:T(1024)(128)(2,1)S(1)}, bf16[4096]{0:T(1024)(128)(2,1)S(1)}) all-reduce(bf16[3072]{0:T(1024)(128)(2,1)S(1)} %dynamic-update-slice, bf16[4096]{0:T(1024)(128)(2,1)S(1)} %dynamic-update-slice.1), channel_id=1, replica_groups=mesh['rep'=2,'fsdp'=64] {'fsdp'}, use_global_device_ids=true, to_apply=%add | all-reduce | flops 7168 | bytes 28672
  521.5 26.0 fusion.59
  547.5 47.2 %multiply_convert_fusion.1 = (bf16[6,197,4096]{2,1,0:T(8,128)(2,1)}, f32[6,197,4096]{2,1,0:T(8,128)}) fusion(f32[6,197,4096]{2,1,0:T(8,128)} %get-tuple-element.69, f32[4096]{0:T(1024)S(1)} %convert_element_type.118, u8[197,4096]{1,0:T(8,128)(4,1)S(1)} %get-tuple-element.20, u8[197,4096]{1,0:T(8,128)(4,1)S(1)} %get-tuple-element.19), kind=kLoop, calls=%fused_computation.13 | loop fusion | flops 343744512 | bytes 50044928 | tf_op jit(solution)/shard_map/convert_element_type | solution.py:43
  594.8 18.1 add_convert_fusion.2
  615.9 142.2 %all-gather.1 = bf16[64,16,8]{1,2,0:T(8,128)(2,1)S(1)} all-gather(bf16[1,16,8]{1,2,0:T(8,128)(2,1)S(1)} %convert_bitcast_fusion), channel_id=1, replica_groups=mesh['rep'=2,'fsdp'=64] {'fsdp'}, dimensions={0}, use_global_device_ids=true | all-gather | bytes 16640 | tf_op jit(solution)/shard_map/all_gather | solution.py:109
  767.8 27.2 fusion.102
  795.0 53.6 %all-gather.21.cloned.1.call-done = bf16[1024,4096]{1,0:T(8,128)(2,1)} async-done(((bf16[16,4096]{1,0:T(8,128)(2,1)}), bf16[1024,4096]{1,0:T(8,128)(2,1)}) %all-gather.21.cloned.1.call-update) | async-done | bytes 8388624 | tf_op jit(solution)/shard_map/all_gather | solution.py:107
  848.7 16.9 fusion.94
  884.4 17.3 convolution_bitcast_fusion
  901.7 13.2 all-gather.23.cloned.1.call-done
  937.0 29.1 %fusion.67 = f32[6,197,1,16,64]{1,4,3,0,2:T(8,128)} fusion(f32[6,16,197,197]{2,3,1,0:T(8,128)} %fusion.60, bf16[6,197,3,16,64]{1,4,3,2,0:T(8,128)(2,1)} %bitcast.156, f32[6,16,197,197]{2,3,1,0:T(8,128)} %get-tuple-element.67, f32[6,16,197]{2,1,0:T(8,128)S(1)} %copy-done.44), kind=kOutput, calls=%fused_computation.97 | convolution fusion | flops 502983744 | bytes 86827008 | tf_op jit(solution)/shard_map/shqk,sqhe->skhe/dot_general | solution.py:88
  966.1 29.1 %fusion.64 = f32[6,197,1,16,64]{1,4,3,0,2:T(8,128)} fusion(f32[6,16,197,197]{2,3,1,0:T(8,128)} %fusion.60, bf16[6,197,3,16,64]{1,4,3,2,0:T(8,128)(2,1)} %bitcast.157, f32[6,16,197,197]{2,3,1,0:T(8,128)} %get-tuple-element.67, f32[6,16,197]{2,1,0:T(8,128)S(1)} %copy-done.44), kind=kOutput, calls=%fused_computation.96 | convolution fusion | flops 502983744 | bytes 86827008 | tf_op jit(solution)/shard_map/shqk,skhe->sqhe/dot_general | solution.py:87
  1027.3 17.4 convolution_bitcast_fusion.2
  1045.4 19.0 convolution_bitcast_fusion.1
  1065.9 15.2 fusion.95
  1094.7 207.1 %reduce-scatter.10.cloned.1.call-done = f32[16,1024]{1,0:T(8,128)} async-done(((f32[1024,1024]{1,0:T(8,128)}), f32[16,1024]{1,0:T(8,128)}) %reduce-scatter.10.cloned.1.call-update) | async-done | bytes 65552 | tf_op jit(solution)/shard_map/reduce_scatter | solution.py:118
  1301.8 389.8 %reduce-scatter.14.cloned.1.call-done = f32[64,1024]{1,0:T(8,128)} async-done(((f32[4096,1024]{1,0:T(8,128)}), f32[64,1024]{1,0:T(8,128)}) %reduce-scatter.14.cloned.1.call-update) | async-done | bytes 262160 | tf_op jit(solution)/shard_map/reduce_scatter | solution.py:118
  1691.5 278.8 %reduce-scatter.8.cloned.1.call-done = f32[16,3072]{1,0:T(8,128)} async-done(((f32[1024,3072]{1,0:T(8,128)}), f32[16,3072]{1,0:T(8,128)}) %reduce-scatter.8.cloned.1.call-update) | async-done | bytes 196624 | tf_op jit(solution)/shard_map/reduce_scatter | solution.py:118
  1970.3 344.8 %reduce-scatter.12.cloned.1.call-done = f32[16,4096]{1,0:T(8,128)} async-done(((f32[1024,4096]{1,0:T(8,128)}), f32[16,4096]{1,0:T(8,128)}) %reduce-scatter.12.cloned.1.call-update) | async-done | bytes 262160 | tf_op jit(solution)/shard_map/reduce_scatter | solution.py:118
  2315.2 291.9 %all-reduce.4 = (f32[3072]{0:T(1024)S(1)}, f32[4096]{0:T(1024)S(1)}) all-reduce(f32[3072]{0:T(1024)S(1)} %reduce_sum.225, f32[4096]{0:T(1024)S(1)} %copy-done.24), channel_id=3, replica_groups=mesh['rep'=2,'fsdp'=64] {'fsdp'}, use_global_device_ids=true, to_apply=%region_14.0.clone | all-reduce | flops 7168 | bytes 57344
  2613.1 49.6 %reduce-scatter.16.cloned.1.call-done = f32[16,8]{1,0:T(8,128)} async-done(((f32[1024,8]{1,0:T(8,128)}), f32[16,8]{1,0:T(8,128)}) %reduce-scatter.16.cloned.1.call-update) | async-done | bytes 528
  2663.5 54.7 %all-reduce.5 = (f32[48]{0:T(128)}, f32[64]{0:T(128)}, f32[8,16]{1,0:T(8,128)}) all-reduce(f32[48]{0:T(128)S(1)} %dynamic-slice.3, f32[64]{0:T(128)S(1)} %dynamic-slice.5, f32[8,16]{1,0:T(8,128)S(1)} %copy.88), channel_id=1, replica_groups=mesh['rep'=2,'fsdp'=64] {'rep'}, use_global_device_ids=true, to_apply=%region_15.0 | all-reduce | flops 240 | bytes 1920 | tf_op jit(solution)/shard_map/psum | solution.py:118
  2718.2 18.0 all-reduce.10.cloned.1.call-done
  (199 shorter events, 186.4 us)
Async XLA Ops:
  7.2 454.3 %copy-start.1 = (bf16[6,197,1024]{2,1,0:T(8,128)(2,1)S(1)}, bf16[6,197,1024]{2,1,0:T(8,128)(2,1)}, u32[]{:S(2)}) copy-start(bf16[6,197,1024]{2,1,0:T(8,128)(2,1)} %param.9) | copy-start | bytes 7262212
  7.2 454.3 %all-gather.11.cloned.1.call-start = ((), (), s32[]{:S(2)}) async-start(), calls=%async_computation.5 | async-start | bytes 6389760 | tf_op jit(solution)/shard_map/all_gather | solution.py:107
  9.0 501.3 %all-gather.13.cloned.1.call-start = ((), (), s32[]{:S(2)}) async-start(), calls=%async_computation.6 | async-start | bytes 2129920 | tf_op jit(solution)/shard_map/all_gather | solution.py:107
  10.6 510.9 %all-gather.15.cloned.1.call-start = ((), (), s32[]{:S(2)}) async-start(), calls=%async_computation.7 | async-start | bytes 8519680 | tf_op jit(solution)/shard_map/all_gather | solution.py:107
  12.3 582.5 %all-gather.17.cloned.1.call-start = ((), (), s32[]{:S(2)}) async-start(), calls=%async_computation.8 | async-start | bytes 8519680 | tf_op jit(solution)/shard_map/all_gather | solution.py:107
  14.0 753.9 %all-gather.19.cloned.1.call-start = ((), (), s32[]{:S(2)}) async-start(), calls=%async_computation.9 | async-start | bytes 8519680 | tf_op jit(solution)/shard_map/all_gather | solution.py:107
  16.1 458.5 %copy-start.12 = (f32[6,197]{1,0:T(8,128)}, f32[6,197]{1,0:T(8,128)S(1)}, u32[]{:S(2)}) copy-start(f32[6,197]{1,0:T(8,128)S(1)} %broadcast_multiply_fusion.1) | copy-start | bytes 14188
  19.3 455.4 %copy-start.18 = (f32[6,197]{1,0:T(8,128)}, f32[6,197]{1,0:T(8,128)S(1)}, u32[]{:S(2)}) copy-start(f32[6,197]{1,0:T(8,128)S(1)} %fusion.87) | copy-start | bytes 14188
  171.5 303.1 %copy-start.34 = (f32[1,1024]{1,0:T(1,128)}, f32[1,1024]{1,0:T(1,128)S(1)}, u32[]{:S(2)}) copy-start(f32[1,1024]{1,0:T(1,128)S(1)} %get-tuple-element.61) | copy-start | bytes 12292
  171.5 303.1 %copy-start.36 = (f32[1,1024]{1,0:T(1,128)}, f32[1,1024]{1,0:T(1,128)S(1)}, u32[]{:S(2)}) copy-start(f32[1,1024]{1,0:T(1,128)S(1)} %get-tuple-element.62) | copy-start | bytes 12292
  171.5 349.9 %copy-start.30 = (f32[1,1024]{1,0:T(1,128)}, f32[1,1024]{1,0:T(1,128)S(1)}, u32[]{:S(2)}) copy-start(f32[1,1024]{1,0:T(1,128)S(1)} %get-tuple-element.58) | copy-start | bytes 12292
  171.6 349.9 %copy-start.32 = (f32[1,1024]{1,0:T(1,128)}, f32[1,1024]{1,0:T(1,128)S(1)}, u32[]{:S(2)}) copy-start(f32[1,1024]{1,0:T(1,128)S(1)} %get-tuple-element.59) | copy-start | bytes 12292
  518.5 352.0 %copy-start.14 = (f32[6,197]{1,0:T(8,128)}, f32[6,197]{1,0:T(8,128)S(1)}, u32[]{:S(2)}) copy-start(f32[6,197]{1,0:T(8,128)S(1)} %broadcast_multiply_fusion) | copy-start | bytes 14188
  521.4 349.1 %copy-start.20 = (f32[6,197]{1,0:T(8,128)}, f32[6,197]{1,0:T(8,128)S(1)}, u32[]{:S(2)}) copy-start(f32[6,197]{1,0:T(8,128)S(1)} %fusion.88) | copy-start | bytes 14188
  613.6 235.1 %all-gather.21.cloned.1.call-start = ((), (), s32[]{:S(2)}) async-start(), calls=%async_computation.10 | async-start | bytes 8519680 | tf_op jit(solution)/shard_map/all_gather | solution.py:107
  614.3 300.6 %all-gather.23.cloned.1.call-start = ((), (), s32[]{:S(2)}) async-start(), calls=%async_computation.11 | async-start | bytes 2129920 | tf_op jit(solution)/shard_map/all_gather | solution.py:107
  615.1 450.7 %all-gather.25.cloned.1.call-start = ((), (), s32[]{:S(2)}) async-start(), calls=%async_computation.12 | async-start | bytes 6389760 | tf_op jit(solution)/shard_map/all_gather | solution.py:107
  615.9 685.9 %reduce-scatter.10.cloned.1.call-start = ((), (), s32[]{:S(2)}) async-start(), calls=%async_computation.14 | async-start | bytes 4259840 | tf_op jit(solution)/shard_map/reduce_scatter | solution.py:118
  884.3 807.2 %reduce-scatter.14.cloned.1.call-start = ((), (), s32[]{:S(2)}) async-start(), calls=%async_computation.16 | async-start | bytes 17039360 | tf_op jit(solution)/shard_map/reduce_scatter | solution.py:118
  901.7 1068.6 %reduce-scatter.8.cloned.1.call-start = ((), (), s32[]{:S(2)}) async-start(), calls=%async_computation.13 | async-start | bytes 12779520 | tf_op jit(solution)/shard_map/reduce_scatter | solution.py:118
  1044.7 1270.4 %reduce-scatter.12.cloned.1.call-start = ((), (), s32[]{:S(2)}) async-start(), calls=%async_computation.15 | async-start | bytes 17039360 | tf_op jit(solution)/shard_map/reduce_scatter | solution.py:118
  1064.5 1598.2 %reduce-scatter.16.cloned.1.call-start = ((), (), s32[]{:S(2)}) async-start(), calls=%async_computation.17 | async-start | bytes 532480
  1087.0 1228.3 %copy-start.24 = (f32[4096]{0:T(1024)S(1)}, f32[4096]{0:T(1024)}, u32[]{:S(2)}) copy-start(f32[4096]{0:T(1024)} %get-tuple-element.74) | copy-start | bytes 49156
  1087.0 1649.3 %all-reduce.10.cloned.1.call-start = ((), (), s32[]{:S(2)}) async-start(), calls=%async_computation.18 | async-start | bytes 1572864 | tf_op jit(solution)/shard_map/psum | solution.py:118
  (39 other events, 954.6 us)
Sparse Core Ops, SparseCore 0:
  11.4 74.3 all-gather.10
  89.2 62.7 all-gather.12
  155.4 78.1 all-gather.14
  236.9 77.9 all-gather.16
  613.7 154.0 all-gather.18
  771.1 77.5 all-gather.20
  852.1 62.7 all-gather.22
  917.7 70.9 all-gather.24
  991.0 310.6 reduce-scatter.9
  1304.0 387.4 reduce-scatter.13
  1696.2 274.0 reduce-scatter.7
  1972.5 342.5 reduce-scatter.11
  2317.5 345.2 reduce-scatter.15
  2665.2 70.9 all-reduce.9
where the time goes:
time: 2750 us
  waiting for transfers between devices  1360 us (49%)
  blocking collectives  928 us (34%)
  matrix products  297 us (11%)
  other arithmetic  99.5 us (4%)
  local copies, waits for them, and re-layouts  43.2 us (2%)
    reduce_scatter x4, waiting for transfers between devices, total_rows(): lax.psum_scatter(full, 'fsdp', scatter_dimension=0, tiled=True)  1220 us
    unnamed x2, blocking collectives  579 us
    all_gather x2, blocking collectives, gather_weights(): lax.all_gather(vec_params.astype(jnp.bfloat16), 'fsdp', axis=1, tiled=True)  294 us
    all_gather x8, waiting for transfers between devices, full_rows(): lax.all_gather(shard.astype(jnp.bfloat16), 'fsdp', axis=0, tiled=True)  75.6 us
  transfers between devices with their start and end apart: 14, of which 9 were waited for; matrix products, arithmetic and copies ran while one was open for 15% of the time, Pallas kernels for 0%

commit v1 on v0

--- a/solution.py
+++ b/solution.py
@@ -1,6 +1,8 @@
 import jax
 import jax.numpy as jnp
 from jax import lax
+from jax.experimental import pallas as pl
+from jax.experimental.pallas import tpu as pltpu
 from jax.sharding import PartitionSpec as P
 
 HEADS = 16
@@ -100,26 +102,365 @@
     return dx_loc, (grad_w_qkv, grad_b_qkv, grad_w_out, grad_w_up, grad_b_up, grad_w_down, grad_vec)
 
 
+MESH_ID = pl.DeviceIdType.MESH
+ORDERS = ((2, 1, 0), (1, 0, 2), (0, 2, 1))
+PIECE = 512
+
+
+def my_place():
+    rep = lax.axis_index("rep")
+    flat = lax.axis_index("fsdp")
+    return rep, (flat // 16, (flat // 4) % 4, flat % 4)
+
+
+def along(place, dim, shift):
+    moved = list(place)
+    moved[dim] = (place[dim] + shift) % 4
+    return tuple(moved)
+
+
+def flat_of(place):
+    return place[0] * 16 + place[1] * 4 + place[2]
+
+
+def entry_barrier(rep, place):
+    barrier = pltpu.get_barrier_semaphore()
+    for dim in range(3):
+        for shift in (1, 3):
+            pl.semaphore_signal(barrier, inc=1, device_id=(rep, flat_of(along(place, dim, shift))),
+                                device_id_type=MESH_ID)
+    pl.semaphore_signal(barrier, inc=1, device_id=(1 - rep, flat_of(place)), device_id_type=MESH_ID)
+    pl.semaphore_wait(barrier, 7)
+
+
+def spot(place, order, upto, dim_index):
+    index = [None, None, None]
+    for k, dim in enumerate(order):
+        index[dim] = slice(None) if k < upto else (dim_index if k == upto else place[dim])
+    return tuple(index)
+
+
+def gather_kernel(*refs):
+    n_in, n_out = 5, 5
+    shards, fulls = refs[:n_in], refs[n_in:n_in + n_out]
+    own_sem, send_sem, recv_sem, pair_send, pair_recv = refs[n_in + n_out:]
+    rep, place = my_place()
+    entry_barrier(rep, place)
+    lanes = []
+    for item, (which, row, cols, base, order) in enumerate(gather_items()):
+        lanes.append((item, which, row, cols, base, order))
+
+    def window(which, row, cols, base, core):
+        col = pl.multiple_of(core * base[0] + base[1], 128)
+        return pl.ds(row, 16), pl.ds(col, cols)
+
+    copies = {}
+
+    def put(item, slot, src, dst, dim, shift):
+        copy = pltpu.make_async_remote_copy(
+            src_ref=src, dst_ref=dst, send_sem=send_sem.at[item, slot], recv_sem=recv_sem.at[item, slot],
+            device_id=(rep, flat_of(along(place, dim, shift))), device_id_type=MESH_ID)
+        copy.start()
+        copies[item, slot] = copy
+
+    def step(lane, level):
+        item, which, row, cols, base, order = lane
+        rows, columns = window(which, row, cols, base, rep)
+        full = fulls[which]
+        if level == 0:
+            copies[item, "own"] = pltpu.make_async_copy(
+                shards[which].at[rows, columns], full.at[place + (rows, columns)], own_sem.at[item])
+            copies[item, "own"].start()
+            for slot, shift in ((0, 1), (1, 3)):
+                put(item, slot, shards[which].at[rows, columns], full.at[place + (rows, columns)], order[0], shift)
+            return
+        if level == 6:
+            copies[item, 10].wait_recv()
+            copies[item, 11].wait_recv()
+            copy = pltpu.make_async_remote_copy(
+                src_ref=full.at[:, :, :, rows, columns], dst_ref=full.at[:, :, :, rows, columns],
+                send_sem=pair_send.at[item], recv_sem=pair_recv.at[item],
+                device_id=(1 - rep, flat_of(place)), device_id_type=MESH_ID)
+            copy.start()
+            copies[item, "pair"] = copy
+            return
+        phase, second = level // 2, level % 2
+        dim = order[phase]
+        if second:
+            for slot, shift, half in ((0, 1, 0), (1, 3, 8)):
+                copies[item, 4 * phase + slot].wait_recv()
+                from_index = (place[dim] + (4 - shift)) % 4
+                where = spot(place, order, phase, from_index) + (pl.ds(row + half, 8), columns)
+                put(item, 4 * phase + 2 + slot, full.at[where], full.at[where], dim, shift)
+        else:
+            if phase == 1:
+                copies[item, "own"].wait()
+            for slot in (2, 3):
+                copies[item, 4 * (phase - 1) + slot].wait_recv()
+            where = spot(place, order, phase, place[dim]) + (rows, columns)
+            for slot, shift in ((0, 1), (1, 3)):
+                put(item, 4 * phase + slot, full.at[where], full.at[where], dim, shift)
+
+    stage_of = [0 if item < 4 else 1 + (item - 4) // 3 for item in range(len(lanes))]
+    n_stage = max(stage_of) + 1
+    for time in range(n_stage + 6):
+        for stage in range(n_stage):
+            level = time - stage
+            if 0 <= level <= 6:
+                for lane in lanes:
+                    if stage_of[lane[0]] == stage:
+                        step(lane, level)
+    for lane in lanes:
+        item = lane[0]
+        copies[item, "pair"].wait_recv()
+    for lane in lanes:
+        item = lane[0]
+        copies[item, "pair"].wait_send()
+        for slot in range(12):
+            copies[item, slot].wait_send()
+
+
+def gather_items():
+    items = [(0, 0, PIECE, (1536, PIECE * j), ORDERS[j]) for j in range(3)]
+    items.append((4, 0, 128, (128, 0), ORDERS[0]))
+    rest = [(1, 0, PIECE, (512, 0))]
+    rest += [(2, 0, PIECE, (2048, PIECE * j)) for j in range(4)]
+    rest += [(3, 16 * j, PIECE, (512, 0)) for j in range(4)]
+    items += [piece + (ORDERS[k % 3],) for k, piece in enumerate(rest)]
+    return items
+
+
+def gather_call(shards):
+    n = len(gather_items())
+    bf = jnp.bfloat16
+    outs = [jax.ShapeDtypeStruct((4, 4, 4) + s.shape, bf) for s in shards]
+    return pl.pallas_call(
+        gather_kernel, out_shape=outs,
+        in_specs=[pl.BlockSpec(memory_space=pltpu.VMEM)] * 5,
+        out_specs=[pl.BlockSpec(memory_space=pl.ANY)] * 5,
+        scratch_shapes=[pltpu.SemaphoreType.DMA((n,)), pltpu.SemaphoreType.DMA((n, 12)),
+                        pltpu.SemaphoreType.DMA((n, 12)), pltpu.SemaphoreType.DMA((n,)),
+                        pltpu.SemaphoreType.DMA((n,))],
+        compiler_params=pltpu.CompilerParams(collective_id=0, has_side_effects=True),
+        name="gather_params",
+    )(*shards)
+
+
+def scatter_items():
+    rest = [(3, 16 * j, PIECE, (512, 0)) for j in range(4)]
+    rest += [(2, 0, PIECE, (2048, PIECE * j)) for j in range(4)]
+    rest += [(1, 0, PIECE, (512, 0))]
+    rest += [(0, 0, PIECE, (1536, PIECE * j)) for j in range(3)]
+    items = [piece + (ORDERS[k % 3],) for k, piece in enumerate(rest)]
+    items.append((4, 0, 128, (128, 0), ORDERS[0]))
+    return items
+
+
+def scatter_kernel(*refs):
+    grads, outs = refs[:5], refs[5:10]
+    pair_buf, pair_small = refs[10:12]
+    (acc, acc_s, stage_buf, stage_s, half0, half1, half2, whole0, whole1, whole2,
+     sh0, sh1, sh2, sw0, sw1, sw2,
+     own_sem, stage_sem, pair_send, pair_recv, send_sem, recv_sem, out_sem, outr_send, outr_recv) = refs[12:]
+    rep, place = my_place()
+    items = scatter_items()
+    n = len(items)
+    small = n - 1
+    copies = {}
+
+    def window(item, core):
+        which, row, cols, base, order = items[item]
+        col = pl.multiple_of(core * base[0] + base[1], 128)
+        return pl.ds(row, 16), pl.ds(col, cols)
+
+    for item in range(n):
+        which = items[item][0]
+        rows, columns = window(item, rep)
+        dst = acc_s if item == small else acc.at[item]
+        copies[item, "own"] = pltpu.make_async_copy(grads[which].at[:, :, :, rows, columns], dst, own_sem.at[item])
+        copies[item, "own"].start()
+    entry_barrier(rep, place)
+    for item in range(n):
+        which = items[item][0]
+        rows, columns = window(item, 1 - rep)
+        dst = pair_small if item == small else pair_buf.at[item]
+        copies[item, "pair"] = pltpu.make_async_remote_copy(
+            src_ref=grads[which].at[:, :, :, rows, columns], dst_ref=dst,
+            send_sem=pair_send.at[item], recv_sem=pair_recv.at[item],
+            device_id=(1 - rep, flat_of(place)), device_id_type=MESH_ID)
+        copies[item, "pair"].start()
+
+    halves, wholes = (half0, half1, half2), (whole0, whole1, whole2)
+    small_halves, small_wholes = (sh0, sh1, sh2), (sw0, sw1, sw2)
+
+    def bufs(item, phase, second, side):
+        if item == small:
+            return (small_wholes if second else small_halves)[phase].at[side]
+        return (wholes if second else halves)[phase].at[item, side]
+
+    def total(item):
+        return acc_s if item == small else acc.at[item]
+
+    def left_over(order, phase):
+        return sorted(order[phase + 1:])
+
+    def index_of(order, phase, dim_index, i):
+        index = list(place)
+        index[order[phase]] = dim_index
+        rest = left_over(order, phase)
+        if len(rest) == 2:
+            index[rest[0]], index[rest[1]] = i // 4, i % 4
+        elif len(rest) == 1:
+            index[rest[0]] = i
+        sub = (i // 4, i % 4) if len(rest) == 2 else ((i,) if len(rest) == 1 else ())
+        return tuple(index), sub
+
+    def piece_of(order, phase, dim_index):
+        index = list(place)
+        index[order[phase]] = dim_index
+        for dim in left_over(order, phase):
+            index[dim] = slice(None)
+        return tuple(index)
+
+    def put(item, slot, src, dst, dim, shift):
+        copy = pltpu.make_async_remote_copy(
+            src_ref=src, dst_ref=dst, send_sem=send_sem.at[item, slot], recv_sem=recv_sem.at[item, slot],
+            device_id=(rep, flat_of(along(place, dim, shift))), device_id_type=MESH_ID)
+        copy.start()
+        copies[item, slot] = copy
+
+    def add(item, phase, dim_index, second, sides, row, rows):
+        order = items[item][4]
+        count = 4 ** (2 - phase)
+
+        def body(i, carry):
+            index, sub = index_of(order, phase, dim_index, i)
+            target = total(item)
+            value = target[index + (pl.ds(row, rows), slice(None))]
+            for side in sides:
+                value = value + bufs(item, phase, second, side)[sub + (slice(None), slice(None))]
+            target[index + (pl.ds(row, rows), slice(None))] = value
+            return carry
+
+        lax.fori_loop(0, count, body, 0)
+
+    def close_phase(item, phase):
+        dim = items[item][4][phase]
+        copies[item, 4 * phase + 2].wait_recv()
+        copies[item, 4 * phase + 3].wait_recv()
+        add(item, phase, place[dim], 1, (0, 1), 0, 16)
+
+    def step(item, level):
+        which, row, cols, base, order = items[item]
+        if level == 0:
+            copies[item, "pair"].wait_recv()
+            stg = stage_s if item == small else stage_buf.at[item % 3]
+            src = pair_small if item == small else pair_buf.at[item]
+            load = pltpu.make_async_copy(src, stg, stage_sem.at[3 if item == small else item % 3])
+            load.start()
+            copies[item, "own"].wait()
+            load.wait()
+
+            def body(i, carry):
+                z, y, x = i // 16, (i // 4) % 4, i % 4
+                target = total(item)
+                target[z, y, x] = target[z, y, x] + stg[z, y, x]
+                return carry
+
+            lax.fori_loop(0, 64, body, 0)
+        if level in (2, 4, 6):
+            close_phase(item, level // 2 - 1)
+        if level == 6:
+            rows, columns = window(item, rep)
+            final = total(item).at[place]
+            out_at = outs[which].at[rows, columns]
+            copies[item, "out"] = pltpu.make_async_copy(final, out_at, out_sem.at[item])
+            copies[item, "out"].start()
+            copies[item, "outr"] = pltpu.make_async_remote_copy(
+                src_ref=final, dst_ref=out_at, send_sem=outr_send.at[item], recv_sem=outr_recv.at[item],
+                device_id=(1 - rep, flat_of(place)), device_id_type=MESH_ID)
+            copies[item, "outr"].start()
+            return
+        phase, second = level // 2, level % 2
+        dim = order[phase]
+        for side, shift, half in ((0, 1, 0), (1, 3, 8)):
+            slot = 4 * phase + 2 * second + side
+            near = (place[dim] + shift) % 4
+            if second:
+                copies[item, 4 * phase + side].wait_recv()
+                add(item, phase, near, 0, (side,), half, 8)
+        for side, shift, half in ((0, 1, 0), (1, 3, 8)):
+            slot = 4 * phase + 2 * second + side
+            near, far = (place[dim] + shift) % 4, (place[dim] + 2) % 4
+            if second:
+                src = total(item).at[piece_of(order, phase, near)]
+            else:
+                src = total(item).at[piece_of(order, phase, far) + (pl.ds(half, 8), slice(None))]
+            put(item, slot, src, bufs(item, phase, second, side), dim, shift)
+
+    stage_of = [item // 3 if item < small else 3 for item in range(n)]
+    n_stage = max(stage_of) + 1
+    for time in range(n_stage + 6):
+        for stage in range(n_stage):
+            level = time - stage
+            if 0 <= level <= 6:
+                for item in range(n):
+                    if stage_of[item] == stage:
+                        step(item, level)
+    for item in range(n):
+        copies[item, "outr"].wait_recv()
+        copies[item, "outr"].wait_send()
+        copies[item, "out"].wait()
+        copies[item, "pair"].wait_send()
+        for slot in range(12):
+            copies[item, slot].wait_send()
+
+
+def scatter_call(grads):
+    n = len(scatter_items())
+    m = n - 1
+    f32 = jnp.float32
+    dma = pltpu.SemaphoreType.DMA
+    outs = [jax.ShapeDtypeStruct(g.shape[3:], f32) for g in grads]
+    outs += [jax.ShapeDtypeStruct((m, 4, 4, 4, 16, PIECE), f32), jax.ShapeDtypeStruct((4, 4, 4, 16, 128), f32)]
+    results = pl.pallas_call(
+        scatter_kernel, out_shape=outs,
+        in_specs=[pl.BlockSpec(memory_space=pl.ANY)] * 5,
+        out_specs=[pl.BlockSpec(memory_space=pl.ANY)] * 7,
+        scratch_shapes=[
+            pltpu.VMEM((m, 4, 4, 4, 16, PIECE), f32), pltpu.VMEM((4, 4, 4, 16, 128), f32),
+            pltpu.VMEM((3, 4, 4, 4, 16, PIECE), f32), pltpu.VMEM((4, 4, 4, 16, 128), f32),
+            pltpu.VMEM((m, 2, 4, 4, 8, PIECE), f32), pltpu.VMEM((m, 2, 4, 8, PIECE), f32), pltpu.VMEM((m, 2, 8, PIECE), f32),
+            pltpu.VMEM((m, 2, 4, 4, 16, PIECE), f32), pltpu.VMEM((m, 2, 4, 16, PIECE), f32), pltpu.VMEM((m, 2, 16, PIECE), f32),
+            pltpu.VMEM((2, 4, 4, 8, 128), f32), pltpu.VMEM((2, 4, 8, 128), f32), pltpu.VMEM((2, 8, 128), f32),
+            pltpu.VMEM((2, 4, 4, 16, 128), f32), pltpu.VMEM((2, 4, 16, 128), f32), pltpu.VMEM((2, 16, 128), f32),
+            dma((n,)), dma((4,)), dma((n,)), dma((n,)), dma((n, 12)), dma((n, 12)), dma((n,)), dma((n,)), dma((n,))],
+        compiler_params=pltpu.CompilerParams(collective_id=1, has_side_effects=True, vmem_limit_bytes=67043328),
+        name="scatter_grads",
+    )(*grads)
+    return results[:5]
+
+
 def gather_weights(shards):
-    w_qkv, b_qkv, w_out, w_up, b_up, w_down, vec_params = shards
-
-    def full_rows(shard):
-        return lax.all_gather(shard.astype(jnp.bfloat16), "fsdp", axis=0, tiled=True)
-
-    vec_full = lax.all_gather(vec_params.astype(jnp.bfloat16), "fsdp", axis=1, tiled=True)
-    return (full_rows(w_qkv), full_rows(b_qkv).astype(jnp.float32), full_rows(w_out), full_rows(w_up),
-            full_rows(b_up).astype(jnp.float32), full_rows(w_down), vec_full.astype(jnp.float32))
+    w_qkv, b_qkv, w_out, w_up, b_up, w_down, vec_params = [s.astype(jnp.bfloat16) for s in shards]
+    small = jnp.zeros((16, 256), jnp.bfloat16)
+    small = small.at[0, 0:48].set(b_qkv).at[0, 48:112].set(b_up).at[0, 128:256].set(vec_params.reshape(128))
+    qkv, out, up, down, table = gather_call((w_qkv, w_out, w_up, w_down, small))
+    table = table.reshape(64, 16, 256)[:, 0].astype(jnp.float32)
+    vec = table[:, 128:].reshape(64, 8, 16).transpose(1, 0, 2).reshape(8, 1024)
+    return (qkv.reshape(1024, 3072), table[:, 0:48].reshape(3072), out.reshape(1024, 1024),
+            up.reshape(1024, 4096), table[:, 48:112].reshape(4096), down.reshape(4096, 1024), vec)
 
 
 def reduce_grads(local_grads):
     grad_w_qkv, grad_b_qkv, grad_w_out, grad_w_up, grad_b_up, grad_w_down, grad_vec = local_grads
-
-    def total_rows(full):
-        return lax.psum(lax.psum_scatter(full, "fsdp", scatter_dimension=0, tiled=True), "rep")
-
-    vec_total = lax.psum(lax.psum_scatter(grad_vec, "fsdp", scatter_dimension=1, tiled=True), "rep")
-    return (total_rows(grad_w_qkv), total_rows(grad_b_qkv), total_rows(grad_w_out), total_rows(grad_w_up),
-            total_rows(grad_b_up), total_rows(grad_w_down), vec_total)
+    flat = jnp.concatenate([grad_b_qkv.reshape(64, 48), grad_b_up.reshape(64, 64), jnp.zeros((64, 16), jnp.float32),
+                            grad_vec.reshape(8, 64, 16).transpose(1, 0, 2).reshape(64, 128)], axis=1)
+    small = jnp.pad(flat[:, None, :], ((0, 0), (0, 15), (0, 0))).reshape(4, 4, 4, 16, 256)
+    qkv, out, up, down, small = scatter_call((
+        grad_w_qkv.reshape(4, 4, 4, 16, 3072), grad_w_out.reshape(4, 4, 4, 16, 1024),
+        grad_w_up.reshape(4, 4, 4, 16, 4096), grad_w_down.reshape(4, 4, 4, 64, 1024), small))
+    return qkv, small[0, 0:48], out, up, small[0, 48:112], down, small[0, 128:256].reshape(8, 16)
 
 
 def solution(mesh):
@@ -130,12 +471,9 @@
     param_specs = (row_spec, flat_spec, row_spec, row_spec, flat_spec, row_spec, col_spec)
 
     def device_step(x_loc, dz_loc, w_qkv, b_qkv, w_out, w_up, b_up, w_down, vec_params):
-        shards = (w_qkv, b_qkv, w_out, w_up, b_up, w_down, vec_params)
-        weights_fwd = gather_weights(shards)
-        z_loc, saved = layer_forward(x_loc, weights_fwd)
-        shards_bwd = lax.optimization_barrier((shards, z_loc))[0]
-        weights_bwd = gather_weights(shards_bwd)
-        dx_loc, local_grads = layer_backward(x_loc, dz_loc, saved, weights_bwd)
+        weights = gather_weights((w_qkv, b_qkv, w_out, w_up, b_up, w_down, vec_params))
+        z_loc, saved = layer_forward(x_loc, weights)
+        dx_loc, local_grads = layer_backward(x_loc, dz_loc, saved, weights)
         return (z_loc, dx_loc) + reduce_grads(local_grads)
 
     return jax.shard_map(device_step, mesh=mesh, in_specs=(batch_spec, batch_spec) + param_specs,

time: 2750 us -> 676 us (0.25)
  waiting for transfers between devices: 1360 us -> 0 us
  blocking collectives: 928 us -> 0 us
  Pallas kernels: 0 us -> 197 us
    reduce_scatter x4 -> x0, waiting for transfers between devices: 1220 us -> none  [total_rows(): lax.psum_scatter(full, 'fsdp', scatter_dimension=0, tiled=True)]
    unnamed x2 -> x0, blocking collectives: 579 us -> none
    all_gather x2 -> x0, blocking collectives: 294 us -> none  [gather_weights(): lax.all_gather(vec_params.astype(jnp.bfloat16), 'fsdp', axis=1, tiled=True)]
    pallas_call x0 -> x2, Pallas kernels: none -> 197 us  [the longest x1 123 us: scatter_call(): pl.pallas_call(scatter_kernel, out_shape=outs, in_specs=[pl.BlockSpec(mem...]
    all_gather x8 -> x0, waiting for transfers between devices: 75.6 us -> none  [full_rows(): lax.all_gather(shard.astype(jnp.bfloat16), 'fsdp', axis=0, tiled=True)]
    psum x1 -> x0, blocking collectives: 54.7 us -> none  [total_rows(): lax.psum(lax.psum_scatter(full, 'fsdp', scatter_dimension=0, tiled=True),...]
    unnamed x15 -> x0, waiting for transfers between devices: 49.9 us -> none
  transfers between devices with their start and end apart: 14 -> 0, of which waited for: 9 -> 0; matrix products, arithmetic and copies ran while one was open for 15% -> 0% of each run, Pallas kernels for 0% -> 0%
where the time goes in v1:
time: 676 us; the launch traced here: 666 us
  matrix products  301 us (45%)
  Pallas kernels  197 us (29%)
  other arithmetic  101 us (15%)
  local copies, waits for them, and re-layouts  64.7 us (10%)
    pallas_call x1, Pallas kernels, scatter_call(): pl.pallas_call(scatter_kernel, out_shape=outs, in_specs=[pl.BlockSpec(mem...  123 us
    pallas_call x1, Pallas kernels, gather_call(): pl.pallas_call(gather_kernel, out_shape=outs, in_specs=[pl.BlockSpec(memo...  73.9 us
    convert_element_type x1, other arithmetic, layer_forward(): mlp_act = gelu_exact(pre_act).astype(jnp.bfloat16)  47.5 us
    dot_general x1, matrix products, layer_backward(): jnp.einsum('shqk,sqhe->skhe', d_scores_bf, q_heads, preferred_element_typ...  29.1 us
    dot_general x1, matrix products, layer_backward(): jnp.einsum('shqk,skhe->sqhe', d_scores_bf, k_heads, preferred_element_typ...  29.1 us
    dot_general x1, matrix products, layer_backward(): jnp.einsum('std,fd->stf', d_mlp_bf, w_down, preferred_element_type=jnp.fl...  27 us
    dot_general x1, matrix products, layer_forward(): jnp.einsum('std,df->stf', h_two, w_up, preferred_element_type=jnp.float32)  25.6 us
    dot_general x1, matrix products, layer_forward(): jnp.einsum('stf,fd->std', mlp_act, w_down, preferred_element_type=jnp.flo...  22.5 us

profile of v1, /device:TPU:1, one launch (start us, length us, event | category | flops | bytes accessed | tf_op | source)
XLA Modules:
  0.0 665.8 jit_solution(15324586545116182016)
XLA Ops:
  20.5 73.9 %gather_params.1 = (bf16[4,4,4,16,3072]{4,3,2,1,0:T(8,128)(2,1)}, bf16[4,4,4,16,1024]{4,3,2,1,0:T(8,128)(2,1)}, bf16[4,4,4,16,4096]{4,3,2,1,0:T(8,128)(2,1)}, bf...) custom-call(bf16[16,3072]{1,0:T(8,128)(2,1)} %convert_element_type.95.refs_0_, ...), custom_call_target="tpu_custom_call" | custom-call | tf_op jit(solution)/shard_map/gather_params/pallas_call | solution.py:237
  103.2 13.6 %add_convert_fusion = bf16[6,197,3072]{2,1,0:T(8,128)(2,1)} fusion(f32[3072]{0:T(1024)S(1)} %add.108, bf16[1024,3072,1]{1,0,2:T(8,128)(2,1)} %bitcast.164, bf16[6,197,1024]{2,1,0:T(8,128)(2,1)} %param.15, f32[1024]{0:T(1024)S(1)} %add.105, f32[1024]{0:T(1024)S(1)} %mul.207, f32[6,197]{1,0:T(8,128)S(1)} %fusion.80, f32[6,197]{1,0:T(8,128)S(1)} %broadcast_multiply_fusion.1), kind=kOutput, calls=%fused_computation.30 | convolution fusion | flops 7451025408 | bytes 16004336 | tf_op jit(solution)/shard_map/std,de->ste/dot_general | solution.py:31
  116.8 11.4 %copy.96 = bf16[6,197,3072]{1,2,0:T(8,128)(2,1)} copy(bf16[6,197,3072]{2,1,0:T(8,128)(2,1)} %add_convert_fusion) | data formatting | bytes 14524416 | tf_op jit(solution)/shard_map/convert_element_type | solution.py:32
  128.2 13.4 %fusion.94 = (f32[6,16,197]{2,1,0:T(8,128)S(1)}, f32[6,16,197,197]{2,3,1,0:T(8,128)}) fusion(bf16[6,197,3,16,64]{1,4,3,2,0:T(8,128)(2,1)} %bitcast.136), kind=kOutput, calls=%fused_computation.142 | convolution fusion | flops 488062176 | bytes 21269760 | tf_op jit(solution)/shard_map/sub | solution.py:37
  141.7 11.4 %fusion.64 = bf16[6,16,64,197]{3,2,1,0:T(8,128)(2,1)} fusion(bf16[6,197,3,16,64]{1,4,3,2,0:T(8,128)(2,1)} %bitcast.137, f32[6,16,197,197]{2,3,1,0:T(8,128)} %get-tuple-element.103, f32[6,16,197]{2,1,0:T(8,128)S(1)} %get-tuple-element.102), kind=kOutput, calls=%fused_computation.92 | convolution fusion | flops 485546688 | bytes 25302912 | tf_op jit(solution)/shard_map/shqk,skhe->sqhe/dot_general | solution.py:39
  153.1 7.6 %fusion.90 = (f32[6,197]{1,0:T(8,128)S(1)}, f32[6,197,1024]{2,1,0:T(8,128)}, f32[6,197,1024]{2,1,0:T(8,128)}) fusion(f32[1024]{0:T(1024)S(1)} %add.111, f32[1024]{0:T(1024)S(1)} %mul.202, bf16[6,197,1024]{2,1,0:T(8,128)(2,1)S(1)} %copy-done, bf16[6,197,1024]{1,2,0:T(8,128)(2,1)} %bitcast.168, bf16[1024,1024,1]{1,0,2:T(8,128)(2,1)S(1)} %bitcast.167), kind=kOutput, calls=%fused_computation.138 | convolution fusion | flops 2484884224 | bytes 16634488 | tf_op jit(solution)/shard_map/std,de->ste/dot_general | solution.py:41
  164.3 25.6 %fusion.48 = (u8[197,4096]{1,0:T(8,128)(4,1)S(1)}, u8[197,4096]{1,0:T(8,128)(4,1)S(1)}, f32[6,197,4096]{2,1,0:T(8,128)}) fusion(f32[4096]{0:T(1024)S(1)} %add.119, bf16[1024,4096,1]{1,0,2:T(8,128)(2,1)} %bitcast.162, f32[6,197,1024]{2,1,0:T(8,128)} %get-tuple-element.83, f32[1024]{0:T(1024)S(1)} %add.116, f32[1024]{0:T(1024)S(1)} %mul.217, ...), kind=kOutput, calls=%fused_computation.77 | convolution fusion | flops 9987553280 | bytes 34243824 | tf_op jit(solution)/shard_map/std,df->stf/dot_general | solution.py:44
  189.9 47.5 %multiply_convert_fusion.1 = (bf16[6,197,4096]{2,1,0:T(8,128)(2,1)}, f32[6,197,4096]{2,1,0:T(8,128)}) fusion(f32[6,197,4096]{2,1,0:T(8,128)} %get-tuple-element.105, f32[4096]{0:T(1024)S(1)} %add.119, u8[197,4096]{1,0:T(8,128)(4,1)S(1)} %get-tuple-element.66, u8[197,4096]{1,0:T(8,128)(4,1)S(1)} %get-tuple-element.65), kind=kLoop, calls=%fused_computation.13 | loop fusion | flops 343744512 | bytes 50044928 | tf_op jit(solution)/shard_map/convert_element_type | solution.py:45
  237.4 27.0 %fusion.95 = (f32[4096]{0:T(1024)}, bf16[6,197,4096]{2,1,0:T(8,128)(2,1)}) fusion(f32[6,197,4096]{2,1,0:T(8,128)} %get-tuple-element.81, bf16[4096,1024,1]{1,0,2:T(8,128)(2,1)} %bitcast.160, bf16[6,197,1024]{2,1,0:T(8,128)(2,1)S(1)} %copy-done.33, f32[1024]{0:T(1024)S(1)} %mul.212, f32[6,197,4096]{2,1,0:T(8,128)} %get-tuple-element.105, f32[4096]{0:T(1024)S(1)} %add.119), kind=kOutput, calls=%fused_computation.143 | convolution fusion | flops 9996425216 | bytes 59260928 | tf_op jit(solution)/shard_map/std,fd->stf/dot_general | solution.py:65
  264.4 18.5 %fusion.87 = (f32[1024]{0:T(1024)}, f32[6,197]{1,0:T(8,128)S(1)}, f32[6,197,1024]{2,1,0:T(8,128)}) fusion(f32[1024]{0:T(1024)S(1)} %mul.217, f32[6,197,1024]{2,1,0:T(8,128)} %get-tuple-element.83, f32[6,197]{1,0:T(8,128)S(1)} %broadcast_multiply_fusion, bf16[1024,4096,1]{1,0,2:T(8,128)(2,1)} %bitcast.163, bf16[6,197,4096]{2,1,0:T(8,128)(2,1)} %get-tuple-element.109), kind=kOutput, calls=%fused_computation.136 | convolution fusion | flops 9921384448 | bytes 27772144 | tf_op jit(solution)/shard_map/stf,df->std/dot_general | solution.py:70
  289.5 22.5 %fusion.38 = (f32[1024]{0:T(1024)}, f32[1024]{0:T(1024)}, bf16[6,197,1024]{2,1,0:T(8,128)(2,1)}, f32[1024]{0:T(1024)}, f32[1024]{0:T(1024)}, /*index=5*/f32[6,197,1024]{2,1,0:T(8,128)}) fusion(bf16[6,197,1024]{2,1,0:T(8,128)(2,1)S(1)} %copy-done.33, f32[1024]{0:T(1024)S(1)} %copy-done.30, f32[1024]{0:T(1024)S(1)} %mul.212, ...), kind=kOutput, calls=%fused_computation.60 | convolution fusion | flops 9941958656 | bytes 42334688 | tf_op jit(solution)/shard_map/stf,fd->std/dot_general | solution.py:46
  322.8 12.5 %fusion.53 = f32[6,197,1,16,64]{1,4,3,0,2:T(8,128)} fusion(bf16[6,197,16,64]{1,3,2,0:T(8,128)(2,1)S(1)} %bitcast.141, f32[6,16,197,197]{2,3,1,0:T(8,128)} %get-tuple-element.103, f32[6,16,197]{2,1,0:T(8,128)S(1)} %get-tuple-element.102), kind=kOutput, calls=%fused_computation.87 | convolution fusion | flops 484336320 | bytes 22240512 | tf_op jit(solution)/shard_map/shqk,sqhe->skhe/dot_general | solution.py:86
  335.3 11.4 %fusion.52 = f32[6,16,197,197]{2,3,1,0:T(8,128)} fusion(bf16[6,197,16,64]{1,3,2,0:T(8,128)(2,1)S(1)} %bitcast.142, bf16[6,197,3,16,64]{1,4,3,2,0:T(8,128)(2,1)} %bitcast.138), kind=kOutput, calls=%fused_computation.86 | convolution fusion | flops 476884992 | bytes 20469120 | tf_op jit(solution)/shard_map/sqhe,skhe->shqk/dot_general | solution.py:85
  346.7 29.1 %fusion.59 = f32[6,197,1,16,64]{1,4,3,0,2:T(8,128)} fusion(f32[6,16,197,197]{2,3,1,0:T(8,128)} %fusion.52, bf16[6,197,3,16,64]{1,4,3,2,0:T(8,128)(2,1)} %bitcast.139, f32[6,16,197,197]{2,3,1,0:T(8,128)} %get-tuple-element.103, f32[6,16,197]{2,1,0:T(8,128)S(1)} %get-tuple-element.102), kind=kOutput, calls=%fused_computation.89 | convolution fusion | flops 502983744 | bytes 86827008 | tf_op jit(solution)/shard_map/shqk,sqhe->skhe/dot_general | solution.py:90
  375.8 29.1 %fusion.56 = f32[6,197,1,16,64]{1,4,3,0,2:T(8,128)} fusion(f32[6,16,197,197]{2,3,1,0:T(8,128)} %fusion.52, bf16[6,197,3,16,64]{1,4,3,2,0:T(8,128)(2,1)} %bitcast.140, f32[6,16,197,197]{2,3,1,0:T(8,128)} %get-tuple-element.103, f32[6,16,197]{2,1,0:T(8,128)S(1)} %get-tuple-element.102), kind=kOutput, calls=%fused_computation.88 | convolution fusion | flops 502983744 | bytes 86827008 | tf_op jit(solution)/shard_map/shqk,skhe->sqhe/dot_general | solution.py:89
  404.9 10.1 %fusion.11 = bf16[6,197,3,16,64]{1,4,3,0,2:T(8,128)(2,1)} fusion(f32[6,197,1,16,64]{1,4,3,0,2:T(8,128)} %fusion.53, f32[6,197,1,16,64]{1,4,3,0,2:T(8,128)} %fusion.59, f32[6,197,1,16,64]{1,4,3,0,2:T(8,128)} %fusion.56), kind=kLoop, calls=%fused_computation.32 | loop fusion | flops 7262208 | bytes 21786624 | tf_op jit(solution)/shard_map/convert_element_type | solution.py:93
  415.0 9.3 %copy.112 = bf16[6,197,3,16,64]{1,4,3,2,0:T(8,128)(2,1)} copy(bf16[6,197,3,16,64]{1,4,3,0,2:T(8,128)(2,1)} %fusion.11) | data formatting | bytes 14524416 | tf_op jit(solution)/shard_map/convert_element_type | solution.py:93
  424.4 15.2 %fusion.88 = (f32[1024]{0:T(1024)S(1)}, f32[6,197]{1,0:T(8,128)S(1)}, f32[6,197,1024]{2,1,0:T(8,128)S(1)}) fusion(f32[1024]{0:T(1024)S(1)} %copy-done.11, f32[6,197]{1,0:T(8,128)S(1)} %copy-done.3, bf16[6,197,1024]{2,1,0:T(8,128)(2,1)S(1)} %copy-done.1, bf16[6,197,3072]{1,2,0:T(8,128)(2,1)} %bitcast.149, bf16[1024,3072,1]{1,0,2:T(8,128)(2,1)} %bitcast.165), kind=kOutput, calls=%fused_computation.137 | convolution fusion | flops 7443761152 | bytes 20833520 | tf_op jit(solution)/shard_map/ste,de->std/dot_general | solution.py:95
  450.8 16.5 %convolution_bitcast_fusion = f32[4,4,4,16,3072]{4,3,0,2,1:T(8,128)} fusion(bf16[6,197,3072,1,1,1]{1,2,3,5,4,0:T(8,128)(2,1)} %bitcast.150, bf16[4,4,4,16,6,197]{5,3,2,1,0,4:T(8,128)(2,1)} %bitcast.156), kind=kOutput, calls=%fused_computation.49 | convolution fusion | flops 7436500992 | bytes 22265856 | tf_op jit(solution)/shard_map/std,ste->de/dot_general | solution.py:94
  467.2 10.8 %copy.129.refs_0_ = f32[4,4,4,16,3072]{4,3,2,1,0:T(8,128)} copy(f32[4,4,4,16,3072]{4,3,0,2,1:T(8,128)} %convolution_bitcast_fusion) | data formatting | bytes 25165824 | tf_op jit(solution)/shard_map/std,ste->de/dot_general | solution.py:94
  485.7 17.9 %fusion.39 = f32[1024,4096,1]{1,0,2:T(8,128)} fusion(bf16[6,197,4096]{2,1,0:T(8,128)(2,1)} %get-tuple-element.109, f32[6,197,1024]{2,1,0:T(8,128)S(1)} %bitcast.146, f32[1024]{0:T(1024)S(1)} %copy-done.29, f32[1024]{0:T(1024)S(1)} %copy-done.16, f32[6,197]{1,0:T(8,128)S(1)} %copy-done.14, f32[6,197]{1,0:T(8,128)S(1)} %copy-done.7), kind=kOutput, calls=%fused_computation.65 | convolution fusion | flops 9921386496 | bytes 31319280 | tf_op jit(solution)/shard_map/std,stf->df/dot_general | solution.py:69
  503.7 17.3 %fusion.67 = f32[4096,1024,1]{1,0,2:T(8,128)} fusion(bf16[6,197,4096]{2,1,0:T(8,128)(2,1)} %get-tuple-element.80, bf16[6,197,1024]{2,1,0:T(8,128)(2,1)S(1)} %copy-done.34, f32[1024]{0:T(1024)S(1)} %copy-done.22), kind=kOutput, calls=%fused_computation.93 | convolution fusion | flops 9918965760 | bytes 28884992 | tf_op jit(solution)/shard_map/stf,std->fd/dot_general | solution.py:64
  522.4 7.7 %fusion.10 = f32[3,16,64]{2,1,0:T(8,128)S(1)} fusion(f32[6,197,1,16,64]{1,4,3,0,2:T(8,128)} %fusion.53, f32[6,197,1,16,64]{1,4,3,0,2:T(8,128)} %fusion.59, f32[6,197,1,16,64]{1,4,3,0,2:T(8,128)} %fusion.56), kind=kLoop, calls=%fused_computation.31 | loop fusion | flops 10890240 | bytes 14536704 | tf_op jit(solution)/shard_map/reduce_sum | solution.py:92
  531.7 123.4 %scatter_grads.1 = (f32[16,3072]{1,0:T(8,128)}, f32[16,1024]{1,0:T(8,128)}, f32[16,4096]{1,0:T(8,128)}, f32[64,1024]{1,0:T(8,128)}, f32[16,256]{1,0:T(8,128)}, /...) custom-call(f32[4,4,4,16,3072]{4,3,2,1,0:T(8,128)} %copy.129.refs_0_, ...), custom_call_target="tpu_custom_call" | custom-call | tf_op jit(solution)/shard_map/scatter_grads/pallas_call | solution.py:426
  (197 shorter events, 81.3 us)
Async XLA Ops:
  96.5 193.0 %copy-start.21 = (f32[1024]{0:T(1024)}, f32[1024]{0:T(1024)S(1)}, u32[]{:S(2)}) copy-start(f32[1024]{0:T(1024)S(1)} %mul.212) | copy-start | bytes 12292
  96.8 215.2 %copy-start.23 = (f32[1024]{0:T(1024)}, f32[1024]{0:T(1024)S(1)}, u32[]{:S(2)}) copy-start(f32[1024]{0:T(1024)S(1)} %mul.202) | copy-start | bytes 12292
  97.2 19.7 %copy-start.19 = (f32[1024]{0:T(1024)}, f32[1024]{0:T(1024)S(1)}, u32[]{:S(2)}) copy-start(f32[1024]{0:T(1024)S(1)} %add.105) | copy-start | bytes 12292
  97.3 19.5 %copy-start.10 = (f32[1024]{0:T(1024)}, f32[1024]{0:T(1024)S(1)}, u32[]{:S(2)}) copy-start(f32[1024]{0:T(1024)S(1)} %mul.207) | copy-start | bytes 12292
  160.8 128.6 %copy-start.15 = (f32[1024]{0:T(1024)}, f32[1024]{0:T(1024)S(1)}, u32[]{:S(2)}) copy-start(f32[1024]{0:T(1024)S(1)} %mul.217) | copy-start | bytes 12292
  160.9 128.6 %copy-start.6 = (f32[6,197]{1,0:T(8,128)}, f32[6,197]{1,0:T(8,128)S(1)}, u32[]{:S(2)}) copy-start(f32[6,197]{1,0:T(8,128)S(1)} %broadcast_multiply_fusion) | copy-start | bytes 14188
  161.2 28.7 %copy-start.28 = (f32[1024]{0:T(1024)}, f32[1024]{0:T(1024)S(1)}, u32[]{:S(2)}) copy-start(f32[1024]{0:T(1024)S(1)} %add.116) | copy-start | bytes 12292
  164.2 125.2 %copy-start.13 = (f32[6,197]{1,0:T(8,128)}, f32[6,197]{1,0:T(8,128)S(1)}, u32[]{:S(2)}) copy-start(f32[6,197]{1,0:T(8,128)S(1)} %fusion.81) | copy-start | bytes 14188
  189.8 47.6 %copy-start.33 = (bf16[6,197,1024]{2,1,0:T(8,128)(2,1)S(1)}, bf16[6,197,1024]{2,1,0:T(8,128)(2,1)}, u32[]{:S(2)}) copy-start(bf16[6,197,1024]{2,1,0:T(8,128)(2,1)} %param.16) | copy-start | bytes 7262212
  424.3 17.9 %slice-start.4 = ((s8[4915200]{0:T(1024)(128)(4,1)}), s8[4194304]{0:T(1024)(128)(4,1)S(1)}, s32[]{:S(2)}) async-start(s8[4915200]{0:T(1024)(128)(4,1)} %bitcast.151), calls=%async_computation.4 | async-start | bytes 8388608
  424.3 17.9 %slice-start.5 = ((s8[4915200]{0:T(1024)(128)(4,1)}), s8[720896]{0:T(1024)(128)(4,1)S(1)}, s32[]{:S(2)}) async-start(s8[4915200]{0:T(1024)(128)(4,1)} %bitcast.151), calls=%async_computation.5 | async-start | bytes 1441792
  424.4 17.9 %copy-start.20 = (f32[1024]{0:T(1024)S(1)}, f32[1024]{0:T(1024)}, u32[]{:S(2)}) copy-start(f32[1024]{0:T(1024)} %copy-done.19) | copy-start | bytes 12292
  446.2 31.8 %slice-start.6 = ((s8[4915200]{0:T(1024)(128)(4,1)}), s8[720896]{0:T(1024)(128)(4,1)S(1)}, s32[]{:S(2)}) async-start(s8[4915200]{0:T(1024)(128)(4,1)} %bitcast.153), calls=%async_computation.6 | async-start | bytes 1441792
  450.8 27.3 %slice-start.7 = ((s8[4915200]{0:T(1024)(128)(4,1)}), s8[4194304]{0:T(1024)(128)(4,1)S(1)}, s32[]{:S(2)}) async-start(s8[4915200]{0:T(1024)(128)(4,1)} %bitcast.153), calls=%async_computation.7 | async-start | bytes 8388608
  467.2 18.5 %slice-start.2 = ((s8[4915200]{0:T(1024)(128)(4,1)}), s8[720896]{0:T(1024)(128)(4,1)S(1)}, s32[]{:S(2)}) async-start(s8[4915200]{0:T(1024)(128)(4,1)} %bitcast.145), calls=%async_computation.2 | async-start | bytes 1441792
  485.7 17.9 %copy-start.22 = (f32[1024]{0:T(1024)S(1)}, f32[1024]{0:T(1024)}, u32[]{:S(2)}) copy-start(f32[1024]{0:T(1024)} %copy-done.21) | copy-start | bytes 12292
  485.7 17.9 %copy-start.34 = (bf16[6,197,1024]{2,1,0:T(8,128)(2,1)S(1)}, bf16[6,197,1024]{2,1,0:T(8,128)(2,1)}, u32[]{:S(2)}) copy-start(bf16[6,197,1024]{2,1,0:T(8,128)(2,1)} %param.16) | copy-start | bytes 7262212
  503.7 17.7 %copy-start.32 = (f32[1024]{0:T(1024)S(1)}, f32[1024]{0:T(1024)}, u32[]{:S(2)}) copy-start(f32[1024]{0:T(1024)} %get-tuple-element.85) | copy-start | bytes 12292
  503.7 17.8 %copy-start.31 = (f32[1024]{0:T(1024)S(1)}, f32[1024]{0:T(1024)}, u32[]{:S(2)}) copy-start(f32[1024]{0:T(1024)} %get-tuple-element.86) | copy-start | bytes 12292
  503.7 18.0 %copy-start.17 = (f32[1024]{0:T(1024)S(1)}, f32[1024]{0:T(1024)}, u32[]{:S(2)}) copy-start(f32[1024]{0:T(1024)} %get-tuple-element.67) | copy-start | bytes 12292
  503.7 18.1 %copy-start.25 = (f32[1024]{0:T(1024)S(1)}, f32[1024]{0:T(1024)}, u32[]{:S(2)}) copy-start(f32[1024]{0:T(1024)} %get-tuple-element.71) | copy-start | bytes 12292
  503.7 18.3 %copy-start.27 = (f32[1024]{0:T(1024)S(1)}, f32[1024]{0:T(1024)}, u32[]{:S(2)}) copy-start(f32[1024]{0:T(1024)} %get-tuple-element.78) | copy-start | bytes 12292
  503.7 18.4 %copy-start.26 = (f32[1024]{0:T(1024)S(1)}, f32[1024]{0:T(1024)}, u32[]{:S(2)}) copy-start(f32[1024]{0:T(1024)} %get-tuple-element.77) | copy-start | bytes 12292
  503.7 18.6 %copy-start.18 = (f32[4096]{0:T(1024)S(1)}, f32[4096]{0:T(1024)}, u32[]{:S(2)}) copy-start(f32[4096]{0:T(1024)} %get-tuple-element.108) | copy-start | bytes 49156
  (20 other events, 134.9 us)
